TPU v7x, 32 devices: a whole 2x2x4 slice. The times are simulated.
32 devices in a mesh: freq: 8 (over z, x), kgrp: 4 (over y, core).
Axes of the slice: x: 2, y: 2, z: 4, core: 2. Of those that a mesh axis runs over, the one named last changes fastest.
Arguments:
- hamiltonian: float32 [256, 64, 128], P(('freq', 'kgrp')), may hold values from -1 to 1, as said below
- self_energy: float32 [16, 64, 128], P('freq'), may hold values from -0.8 to 0.3, as said below
- guess_factor: float32 [16, 64, 128], P('freq'), may hold values from -0.05 to 1.25
- weights: int32 [256], replicated, may hold values from 1 to 48
- counts: int32 [16], replicated, may hold values from 1 to 3, as said below
Outputs:
- local_green: float32 [4096, 32], P(('freq', 'kgrp'))
Inputs may be any that keep to these rules, and one draw needn't show every extreme that they name: `hamiltonian`: each k-point's matrix is Hermitian: the left half symmetric, the right half antisymmetric. `self_energy`: the diagonal of the right half lies between -0.8 and -0.4. `counts`: the number of Newton-Schulz steps taken at each frequency.
All inputs are finite; a program needn't handle non-finite values.
Results may differ from a plain program's by a relative error of at most 0.0001.
Values sent between devices are 32-bit elements.
A program may use at most 64 MiB of HBM per device.

v0:
```python
import math
import jax
import jax.numpy as jnp
from jax import lax
from jax.sharding import PartitionSpec as P

chem_potential = 0.2


def blockify(right_side):
    order = right_side.shape[-1] // 2
    real_part = right_side[..., :order]
    imag_part = right_side[..., order:]
    upper_row = jnp.concatenate([real_part, imag_part], -1)
    lower_row = jnp.concatenate([-imag_part, real_part], -1)
    return jnp.concatenate([upper_row, lower_row], -2)


def complex_product(left_side, right_side):
    return jnp.einsum(
        "...ij,...jl->...il", left_side, blockify(right_side), precision=lax.Precision.HIGHEST
    )


def build_matrix(kpoint_rows, sigma_rows, matsubara):
    orbitals = kpoint_rows.shape[1]
    identity = jnp.eye(orbitals, dtype=jnp.float32)
    real_shift = jnp.broadcast_to(chem_potential * identity, matsubara.shape + identity.shape)
    imag_shift = matsubara[:, None, None] * identity
    diagonal_shift = jnp.concatenate([real_shift, imag_shift], -1)
    return diagonal_shift[:, None] - kpoint_rows[None] - sigma_rows[:, None]


def start_guess(matrix, factor_rows):
    orbitals = matrix.shape[-2]
    diag_real = jnp.diagonal(matrix[..., :orbitals], axis1=-2, axis2=-1)
    diag_imag = jnp.diagonal(matrix[..., orbitals:], axis1=-2, axis2=-1)
    modulus = diag_real * diag_real + diag_imag * diag_imag
    recip_real = (diag_real / modulus)[..., None]
    recip_imag = (-diag_imag / modulus)[..., None]
    factor_real = factor_rows[..., :orbitals]
    factor_imag = factor_rows[..., orbitals:]
    guess_real = recip_real * factor_real - recip_imag * factor_imag
    guess_imag = recip_real * factor_imag + recip_imag * factor_real
    return jnp.concatenate([guess_real, guess_imag], -1)


def invert_blocks(kpoint_rows, sigma_rows, factor_rows, freq_ids, freq_total, step_counts):
    orbitals = kpoint_rows.shape[1]
    matsubara = (2 * freq_ids + 1).astype(jnp.float32) * (math.pi / (2 * freq_total))
    matrix = build_matrix(kpoint_rows, sigma_rows, matsubara)
    initial = start_guess(matrix, factor_rows[:, None])
    identity = jnp.eye(orbitals, dtype=jnp.float32)
    doubled = jnp.concatenate([2.0 * identity, jnp.zeros_like(identity)], -1)
    longest = jnp.max(step_counts)

    def newton_step(sweep, current):
        updated = complex_product(current, doubled - complex_product(matrix, current))
        active = (sweep < step_counts)[:, None, None, None]
        return jnp.where(active, updated, current)

    return lax.fori_loop(0, longest, newton_step, initial)


def per_device(hamiltonian, self_energy, guess_factor, weights, counts):
    orbitals = hamiltonian.shape[1]
    per_freq = self_energy.shape[0]
    k_local = hamiltonian.shape[0]
    freq_devs = lax.axis_size("freq")
    group_devs = lax.axis_size("kgrp")
    freq_total = per_freq * freq_devs
    pair_block = orbitals * orbitals // (freq_devs * group_devs)
    freq_pos = lax.axis_index("freq")
    group_pos = lax.axis_index("kgrp")
    weight_total = jnp.sum(weights.astype(jnp.float32))
    first_freq = freq_pos * per_freq
    freq_ids = first_freq + jnp.arange(per_freq, dtype=jnp.int32)
    local_counts = lax.dynamic_slice_in_dim(counts, first_freq, per_freq)
    empty = jnp.zeros((per_freq, orbitals, 2 * orbitals), jnp.float32)
    h_piece = lax.all_gather(hamiltonian, "freq", axis=0, tiled=True)
    row_ids = jnp.arange(h_piece.shape[0], dtype=jnp.int32)
    kpoint_ids = (
        row_ids // k_local * (group_devs * k_local) + group_pos * k_local + row_ids % k_local
    )
    factors = jnp.take(weights, kpoint_ids).astype(jnp.float32)
    inverses = invert_blocks(h_piece, self_energy, guess_factor, freq_ids, freq_total, local_counts)
    partial_sum = empty + jnp.einsum(
        "k,fkij->fij", factors, inverses, precision=lax.Precision.HIGHEST
    )
    partial_term = partial_sum.reshape(per_freq, orbitals, 2, orbitals).transpose(0, 2, 1, 3)
    partial_term = partial_term.reshape(per_freq, 2, freq_devs, group_devs, pair_block)
    quarter = lax.psum_scatter(partial_term, "kgrp", scatter_dimension=3, tiled=True)
    own_block = lax.all_to_all(quarter, "freq", split_axis=2, concat_axis=0, tiled=True)
    result = own_block.reshape(freq_total, 2, pair_block).transpose(2, 1, 0)
    result = result.reshape(pair_block, 2 * freq_total)
    return result / weight_total


def solution(mesh):
    return jax.shard_map(
        per_device,
        mesh=mesh,
        in_specs=(
            P(("freq", "kgrp"), None, None),
            P("freq", None, None),
            P("freq", None, None),
            P(),
            P(),
        ),
        out_specs=P(("freq", "kgrp"), None),
        check_vma=False,
    )
```

profile of v0, /device:TPU:0, one launch (start us, length us, event | category | flops | bytes accessed | tf_op | source)
XLA Modules:
  0.0 254.6 jit_solution(18190789245727477502)
XLA Ops:
  6.5 0.7 all-gather.2.cloned.1.call-update
  7.3 0.0 reduce-scatter.2.cloned.1.call-start
  7.4 0.1 broadcast_multiply_fusion
  7.4 0.1 pad_maximum_fusion.1
  7.5 0.0 copy-start
  7.6 2.6 %copy.25 = f32[2,64,128]{0,2,1:T(8,128)} copy(f32[2,64,128]{2,1,0:T(8,128)S(1)} %pad_maximum_fusion.1) | data formatting | bytes 131072 | tf_op jit(solution)/shard_map/concatenate | solution.py:30
  10.2 2.6 %copy.27 = f32[2,64,128]{0,2,1:T(8,128)} copy(f32[2,64,128]{2,1,0:T(8,128)S(1)} %copy-done.2) | data formatting | bytes 131072 | tf_op args[1]
  12.8 0.8 gather_fusion
  13.6 0.7 fusion.63
  14.4 0.1 slice_bitcast_fusion.1
  14.5 46.8 %all-gather.2.cloned.1.call-done = f32[64,64,128]{2,1,0:T(8,128)} async-done(((f32[8,64,128]{2,1,0:T(8,128)}), f32[64,64,128]{2,1,0:T(8,128)}) %all-gather.2.cloned.1.call-update) | async-done | bytes 2097168 | tf_op jit(solution)/shard_map/all_gather | solution.py:80
  61.3 3.8 %copy.26 = f32[64,64,128]{0,2,1:T(8,128)} copy(f32[64,64,128]{2,1,0:T(8,128)} %all-gather.2.cloned.1.call-done) | data formatting | bytes 4194304 | tf_op jit(solution)/shard_map/all_gather | solution.py:80
  65.1 22.3 %subtract_subtract_fusion = f32[2,64,64,128]{1,0,3,2:T(2,128)} fusion(f32[2,64,128]{0,2,1:T(8,128)} %copy.27, f32[64,64,128]{0,2,1:T(8,128)} %copy.26, f32[2,64,128]{0,2,1:T(8,128)} %copy.25), kind=kLoop, calls=%fused_computation.30 | loop fusion | flops 2097152 | bytes 6422528 | tf_op jit(solution)/shard_map/sub | solution.py:31
  87.4 7.8 %fusion.64 = (f32[2,64,64,64]{1,0,3,2:T(2,128)}, f32[2,64,64,64]{1,0,3,2:T(2,128)}) fusion(f32[2,64,64,128]{1,0,3,2:T(2,128)} %subtract_subtract_fusion), kind=kLoop, calls=%fused_computation.96 | loop fusion | bytes 8388608 | tf_op jit(solution)/shard_map/slice | solution.py:36
  95.3 2.9 %gather_fusion.1 = f32[64,2,64]{2,1,0:T(2,128)S(1)} fusion(f32[2,64,64,64]{1,0,3,2:T(2,128)} %get-tuple-element.83, s32[64]{0:T(128)S(1)} %or_bitcast_fusion), kind=kCustom, calls=%fused_computation.1 | custom fusion | bytes 66048 | tf_op jit(solution)/shard_map/jit(diagonal)/gather | solution.py:36
  98.2 0.1 copy.28
  98.3 3.0 %gather_fusion.2 = f32[64,2,64]{2,1,0:T(2,128)S(1)} fusion(f32[2,64,64,64]{1,0,3,2:T(2,128)} %get-tuple-element.84, s32[64]{0:T(128)S(1)} %or_bitcast_fusion), kind=kCustom, calls=%fused_computation.2 | custom fusion | bytes 66048 | tf_op jit(solution)/shard_map/jit(diagonal)/gather | solution.py:37
  101.2 0.1 copy.29
  101.4 2.3 multiply_subtract_fusion
  103.7 3.1 %pad_maximum_fusion = f32[2,64,64,128]{3,2,1,0:T(8,128)} fusion(f32[2,64,64,64]{3,2,1,0:T(8,128)S(1)} %get-tuple-element.86, f32[2,64,64,64]{3,2,1,0:T(8,128)S(1)} %get-tuple-element.85), kind=kLoop, calls=%fused_computation.31 | loop fusion | flops 1048576 | bytes 8388608 | tf_op jit(solution)/shard_map/concatenate | solution.py:45
  106.8 87.1 %while.11 = (s32[]{:T(128)}, f32[2,64,64,128]{3,2,1,0:T(8,128)}, s32[]{:T(128)}, s32[2]{0:T(128)S(1)}, f32[64,128]{1,0:T(8,128)S(1)}, /*index=5*/f32[64,64,128]{...) while((s32[]{:T(128)}, f32[2,64,64,128]{3,2,1,0:T(8,128)}, ...), condition=%wide.region_2.3_spmd.clone, body=%wide.region_1.2_spmd.clone.sunk | while | flops 3234856960 | bytes 56787048 | solution.py:62
  107.6 2.2 copy.51
  109.8 1.4 slice_negate_fusion.4
  111.3 8.9 %bitcast_subtract_fusion.2 = f32[2,64,64,128]{3,2,1,0:T(8,128)S(1)} fusion(f32[64,128]{1,0:T(8,128)S(1)} %get-tuple-element.171, f32[2,64,128]{2,1,0:T(8,128)S(1)} %get-tuple-element.174, f32[64,64,128]{2,1,0:T(8,128)S(1)} %get-tuple-element.172, f32[2,64,128]{2,1,0:T(8,128)S(1)} %get-tuple-element.173, ...), kind=kOutput, calls=%fused_computation.18.clone.1 | convolution fusion | flops 1617952768 | bytes 14843904 | tf_op jit(solution)/shard_map/while/body/...ij,...jl->...il/dot_general | solution.py:20
  120.2 3.5 %slice_negate_fusion.5 = (f32[2,64,64,64]{3,2,1,0:T(8,128)S(1)}, f32[2,64,64,64]{3,2,1,0:T(8,128)}) fusion(f32[2,64,64,128]{3,2,1,0:T(8,128)S(1)} %bitcast_subtract_fusion.2), kind=kLoop, calls=%fused_computation.16.clone.1 | loop fusion | flops 524288 | bytes 8388608 | tf_op jit(solution)/shard_map/while/body/neg | solution.py:15
  123.7 11.9 %bitcast_select_fusion.2 = f32[2,64,64,128]{3,2,1,0:T(8,128)} fusion(f32[2,64,64,128]{3,2,1,0:T(8,128)S(1)} %copy.51, f32[2,64,64,64]{3,2,1,0:T(8,128)} %get-tuple-element.147, f32[2,64,64,64]{3,2,1,0:T(8,128)S(1)} %get-tuple-element.148, f32[2,64,64,128]{3,2,1,0:T(8,128)S(1)} %bitcast_subtract_fusion.2, pred[2]{0:T(512)(128)(4,1)S(1)} %broadcast_compare_fusion.2), kind=kOutput, calls=%fused_computation.17.clone.1 | convolution fusion | flops 1615855616 | bytes 16777218 | tf_op jit(solution)/shard_map/while/body/...ij,...jl->...il/dot_general | solution.py:20
  136.3 2.2 copy.51
  138.5 1.4 slice_negate_fusion.4
  139.9 8.9 %bitcast_subtract_fusion.2 = f32[2,64,64,128]{3,2,1,0:T(8,128)S(1)} fusion(f32[64,128]{1,0:T(8,128)S(1)} %get-tuple-element.171, f32[2,64,128]{2,1,0:T(8,128)S(1)} %get-tuple-element.174, f32[64,64,128]{2,1,0:T(8,128)S(1)} %get-tuple-element.172, f32[2,64,128]{2,1,0:T(8,128)S(1)} %get-tuple-element.173, ...), kind=kOutput, calls=%fused_computation.18.clone.1 | convolution fusion | flops 1617952768 | bytes 14843904 | tf_op jit(solution)/shard_map/while/body/...ij,...jl->...il/dot_general | solution.py:20
  148.9 3.5 %slice_negate_fusion.5 = (f32[2,64,64,64]{3,2,1,0:T(8,128)S(1)}, f32[2,64,64,64]{3,2,1,0:T(8,128)}) fusion(f32[2,64,64,128]{3,2,1,0:T(8,128)S(1)} %bitcast_subtract_fusion.2), kind=kLoop, calls=%fused_computation.16.clone.1 | loop fusion | flops 524288 | bytes 8388608 | tf_op jit(solution)/shard_map/while/body/neg | solution.py:15
  152.4 11.9 %bitcast_select_fusion.2 = f32[2,64,64,128]{3,2,1,0:T(8,128)} fusion(f32[2,64,64,128]{3,2,1,0:T(8,128)S(1)} %copy.51, f32[2,64,64,64]{3,2,1,0:T(8,128)} %get-tuple-element.147, f32[2,64,64,64]{3,2,1,0:T(8,128)S(1)} %get-tuple-element.148, f32[2,64,64,128]{3,2,1,0:T(8,128)S(1)} %bitcast_subtract_fusion.2, pred[2]{0:T(512)(128)(4,1)S(1)} %broadcast_compare_fusion.2), kind=kOutput, calls=%fused_computation.17.clone.1 | convolution fusion | flops 1615855616 | bytes 16777218 | tf_op jit(solution)/shard_map/while/body/...ij,...jl->...il/dot_general | solution.py:20
  165.0 2.2 copy.51
  167.2 1.4 slice_negate_fusion.4
  168.6 8.9 %bitcast_subtract_fusion.2 = f32[2,64,64,128]{3,2,1,0:T(8,128)S(1)} fusion(f32[64,128]{1,0:T(8,128)S(1)} %get-tuple-element.171, f32[2,64,128]{2,1,0:T(8,128)S(1)} %get-tuple-element.174, f32[64,64,128]{2,1,0:T(8,128)S(1)} %get-tuple-element.172, f32[2,64,128]{2,1,0:T(8,128)S(1)} %get-tuple-element.173, ...), kind=kOutput, calls=%fused_computation.18.clone.1 | convolution fusion | flops 1617952768 | bytes 14843904 | tf_op jit(solution)/shard_map/while/body/...ij,...jl->...il/dot_general | solution.py:20
  177.6 3.5 %slice_negate_fusion.5 = (f32[2,64,64,64]{3,2,1,0:T(8,128)S(1)}, f32[2,64,64,64]{3,2,1,0:T(8,128)}) fusion(f32[2,64,64,128]{3,2,1,0:T(8,128)S(1)} %bitcast_subtract_fusion.2), kind=kLoop, calls=%fused_computation.16.clone.1 | loop fusion | flops 524288 | bytes 8388608 | tf_op jit(solution)/shard_map/while/body/neg | solution.py:15
  181.1 11.9 %bitcast_select_fusion.2 = f32[2,64,64,128]{3,2,1,0:T(8,128)} fusion(f32[2,64,64,128]{3,2,1,0:T(8,128)S(1)} %copy.51, f32[2,64,64,64]{3,2,1,0:T(8,128)} %get-tuple-element.147, f32[2,64,64,64]{3,2,1,0:T(8,128)S(1)} %get-tuple-element.148, f32[2,64,64,128]{3,2,1,0:T(8,128)S(1)} %bitcast_subtract_fusion.2, pred[2]{0:T(512)(128)(4,1)S(1)} %broadcast_compare_fusion.2), kind=kOutput, calls=%fused_computation.17.clone.1 | convolution fusion | flops 1615855616 | bytes 16777218 | tf_op jit(solution)/shard_map/while/body/...ij,...jl->...il/dot_general | solution.py:20
  193.9 9.2 %dot_general.18 = f32[2,64,2,64,64]{3,2,1,4,0:T(2,128)} reshape(f32[2,64,128,64]{2,1,3,0:T(8,128)} %bitcast.62) | data formatting | bytes 8388608 | tf_op jit(solution)/shard_map/k,fkij->fij/dot_general | solution.py:87
  203.1 12.3 %fusion.27 = f32[1,2,64,2,64]{4,0,3,2,1:T(1,128)S(1)} fusion(f32[2,64,2,64,64]{3,2,1,4,0:T(2,128)} %dot_general.18, s32[64]{0:T(128)S(1)} %gather_fusion, s32[]{:T(128)S(6)} %mul.134), kind=kOutput, calls=%fused_computation.28 | convolution fusion | flops 12584384 | bytes 4260100 | tf_op jit(solution)/shard_map/k,fkij->fij/dot_general | solution.py:87
  215.3 0.1 reshape.121
  215.4 0.6 copy.32
  216.1 0.0 reduce-scatter.2.cloned.1.call-update
  216.1 16.9 %reduce-scatter.2.cloned.1.call-done = f32[2,2,8,1,128]{4,2,1,0,3:T(8,128)} async-done(((f32[2,2,8,4,128]{4,2,1,0,3:T(8,128)}), f32[2,2,8,1,128]{4,2,1,0,3:T(8,128)}) %reduce-scatter.2.cloned.1.call-update) | async-done | bytes 16400 | tf_op jit(solution)/shard_map/reduce_scatter | solution.py:92
  233.0 1.3 copy.33
  234.4 5.5 %all-to-all-start = ((f32[2,2,8,1,128]{4,3,1,0,2:T(1,128)}), f32[2,2,8,1,128]{4,3,1,0,2:T(1,128)S(1)}, u32[]{:S(2)}, u32[]{:S(2)}) async-start(f32[2,2,8,1,128]{4,3,1,0,2:T(1,128)} %copy.33), calls=%async_computation.1 | async-start | bytes 32768 | tf_op jit(solution)/shard_map/all_to_all | solution.py:93
  239.9 0.6 convert_reduce_fusion
  240.5 6.0 %all-to-all-done = f32[2,2,8,1,128]{4,3,1,0,2:T(1,128)S(1)} async-done(((f32[2,2,8,1,128]{4,3,1,0,2:T(1,128)}), f32[2,2,8,1,128]{4,3,1,0,2:T(1,128)S(1)}, u32[]{:S(2)}, u32[]{:S(2)}) %all-to-all-start) | async-done | bytes 16416 | tf_op jit(solution)/shard_map/all_to_all | solution.py:93
  246.5 0.7 broadcast_divide_fusion
  247.1 0.6 copy.34
  (24 shorter events, 0.1 us)
Async XLA Ops:
  6.5 3.6 %copy-start.2 = (f32[2,64,128]{2,1,0:T(8,128)S(1)}, f32[2,64,128]{2,1,0:T(8,128)}, u32[]{:S(2)}) copy-start(f32[2,64,128]{2,1,0:T(8,128)} %param.8) | copy-start | bytes 196612
  6.5 54.8 %all-gather.2.cloned.1.call-start = ((), (), s32[]{:S(2)}) async-start(), calls=%async_computation.2 | async-start | bytes 2359296 | tf_op jit(solution)/shard_map/all_gather | solution.py:80
  7.3 225.8 %reduce-scatter.2.cloned.1.call-start = ((), (), s32[]{:S(2)}) async-start(), calls=%async_computation.3 | async-start | bytes 81920 | tf_op jit(solution)/shard_map/reduce_scatter | solution.py:92
  7.5 5.3 %copy-start = (s32[256]{0:T(256)S(1)}, s32[256]{0:T(256)}, u32[]{:S(2)}) copy-start(s32[256]{0:T(256)} %param.10) | copy-start | bytes 3076
  7.5 6.1 %copy-start.4 = (s32[16]{0:T(128)S(1)}, s32[16]{0:T(128)}, u32[]{:S(2)}) copy-start(s32[16]{0:T(128)} %param.11) | copy-start | bytes 196
  7.6 6.8 %copy-start.3 = (f32[2,64,128]{2,1,0:T(8,128)S(1)}, f32[2,64,128]{2,1,0:T(8,128)}, u32[]{:S(2)}) copy-start(f32[2,64,128]{2,1,0:T(8,128)} %param.9) | copy-start | bytes 196612
  103.7 3.1 %copy-start.1 = (f32[64,64,128]{2,1,0:T(8,128)S(1)}, f32[64,64,128]{2,1,0:T(8,128)}, u32[]{:S(2)}) copy-start(f32[64,64,128]{2,1,0:T(8,128)} %all-gather.2.cloned.1.call-done) | copy-start | bytes 6291460
  234.4 12.1 %all-to-all-start = ((f32[2,2,8,1,128]{4,3,1,0,2:T(1,128)}), f32[2,2,8,1,128]{4,3,1,0,2:T(1,128)S(1)}, u32[]{:S(2)}, u32[]{:S(2)}) async-start(f32[2,2,8,1,128]{4,3,1,0,2:T(1,128)} %copy.33), calls=%async_computation.1 | async-start | bytes 32768 | tf_op jit(solution)/shard_map/all_to_all | solution.py:93
Sparse Core Ops, SparseCore 0:
  9.5 51.7 all-gather.1
  216.2 16.7 reduce-scatter.1
where the time goes:
time: 255 us
  matrix products  74.9 us (29%)
  waiting for transfers between devices  70.5 us (28%)
  other arithmetic  44.8 us (18%)
  local copies, waits for them, and re-layouts  42.3 us (17%)
  between operations  13.6 us (5%)
  starting transfers between devices  5.57 us (2%)
  loops' own time  3.03 us (1%)
    dot_general x6, matrix products, complex_product(): jnp.einsum('...ij,...jl->...il', left_side, blockify(right_side), precisi...  62.6 us
    all_gather x1, waiting for transfers between devices, per_device(): h_piece = lax.all_gather(hamiltonian, 'freq', axis=0, tiled=True)  46.8 us
    sub x1, other arithmetic, build_matrix(): return diagonal_shift[:, None] - kpoint_rows[None] - sigma_rows[:, None]  22.3 us
    reduce_scatter x1, waiting for transfers between devices, per_device(): lax.psum_scatter(partial_term, 'kgrp', scatter_dimension=3, tiled=True)  16.9 us
    neg x6, other arithmetic, blockify(): lower_row = jnp.concatenate([-imag_part, real_part], -1)  14.8 us
    dot_general x1, matrix products, per_device(): jnp.einsum('k,fkij->fij', factors, inverses, precision=lax.Precision.HIGH...  12.3 us
    dot_general x2, local copies, waits for them, and re-layouts, per_device(): jnp.einsum('k,fkij->fij', factors, inverses, precision=lax.Precision.HIGH...  9.2 us
    slice x1, local copies, waits for them, and re-layouts, start_guess(): diag_real = jnp.diagonal(matrix[..., :orbitals], axis1=-2, axis2=-1)  7.83 us
  transfers between devices with their start and end apart: 3, of which 3 were waited for; matrix products, arithmetic and copies ran while one was open for 3% of the time, Pallas kernels for 0%

commit v1 on v0

--- a/solution.py
+++ b/solution.py
@@ -77,7 +77,24 @@
     freq_ids = first_freq + jnp.arange(per_freq, dtype=jnp.int32)
     local_counts = lax.dynamic_slice_in_dim(counts, first_freq, per_freq)
     empty = jnp.zeros((per_freq, orbitals, 2 * orbitals), jnp.float32)
-    h_piece = lax.all_gather(hamiltonian, "freq", axis=0, tiled=True)
+    local_array = hamiltonian
+    taken_in, q_next, res = (lax.axis_size("freq"), lax.axis_index("freq"), local_array.shape[0])
+    h_piece = lax.dynamic_update_slice_in_dim(
+        jnp.zeros(
+            [it * taken_in if nth == 0 else it for nth, it in enumerate(local_array.shape)],
+            local_array.dtype,
+        ),
+        local_array,
+        q_next * res,
+        axis=0,
+    )
+    for num in [*range(1, taken_in)]:
+        local_array = lax.ppermute(
+            local_array, "freq", [(nth, (nth + 1) % taken_in) for nth in range(taken_in)]
+        )
+        h_piece = lax.dynamic_update_slice_in_dim(
+            h_piece, local_array, (q_next - num) % taken_in * res, axis=0
+        )
     row_ids = jnp.arange(h_piece.shape[0], dtype=jnp.int32)
     kpoint_ids = (
         row_ids // k_local * (group_devs * k_local) + group_pos * k_local + row_ids % k_local

time: 255 us -> 269 us (1.055)
  waiting for transfers between devices: 70.5 us -> 78.9 us
  starting transfers between devices: 5.57 us -> 8.47 us
    ppermute x0 -> x7, waiting for transfers between devices: none -> 56.1 us  [per_device(): lax.ppermute(local_array, 'freq', [(nth, (nth + 1) % taken_in) for nth in...]
    all_gather x1 -> x0, waiting for transfers between devices: 46.8 us -> none  [per_device(): h_piece = lax.all_gather(hamiltonian, 'freq', axis=0, tiled=True)]
    dynamic_update_slice x0 -> x9, local copies, waits for them, and re-layouts: none -> 4.83 us  [the longest x8 3.85 us: per_device(): lax.dynamic_update_slice_in_dim(h_piece, local_array, (q_next - num) % ta...]
    all_gather x1 -> x0, local copies, waits for them, and re-layouts: 3.82 us -> none  [per_device(): h_piece = lax.all_gather(hamiltonian, 'freq', axis=0, tiled=True)]
    ppermute x0 -> x7, starting transfers between devices: none -> 2.98 us  [per_device(): lax.ppermute(local_array, 'freq', [(nth, (nth + 1) % taken_in) for nth in...]
  transfers between devices with their start and end apart: 3 -> 9, of which waited for: 3 -> 9; matrix products, arithmetic and copies ran while one was open for 3% -> 4% of each run, Pallas kernels for 0% -> 0%
where the time goes in v1:
time: 269 us; the launch traced here: 268 us
  waiting for transfers between devices  78.9 us (29%)
  matrix products  75.1 us (28%)
  other arithmetic  45.5 us (17%)
  local copies, waits for them, and re-layouts  43.5 us (16%)
  between operations  13.6 us (5%)
  starting transfers between devices  8.47 us (3%)
  loops' own time  3.24 us (1%)
    dot_general x6, matrix products, complex_product(): jnp.einsum('...ij,...jl->...il', left_side, blockify(right_side), precisi...  62.8 us
    ppermute x7, waiting for transfers between devices, per_device(): lax.ppermute(local_array, 'freq', [(nth, (nth + 1) % taken_in) for nth in...  56.1 us
    sub x1, other arithmetic, build_matrix(): return diagonal_shift[:, None] - kpoint_rows[None] - sigma_rows[:, None]  22.3 us
    reduce_scatter x1, waiting for transfers between devices, per_device(): lax.psum_scatter(partial_term, 'kgrp', scatter_dimension=3, tiled=True)  16.8 us
    neg x6, other arithmetic, blockify(): lower_row = jnp.concatenate([-imag_part, real_part], -1)  14.8 us
    dot_general x1, matrix products, per_device(): jnp.einsum('k,fkij->fij', factors, inverses, precision=lax.Precision.HIGH...  12.3 us
    dot_general x2, local copies, waits for them, and re-layouts, per_device(): jnp.einsum('k,fkij->fij', factors, inverses, precision=lax.Precision.HIGH...  9.2 us
    slice x1, local copies, waits for them, and re-layouts, start_guess(): diag_real = jnp.diagonal(matrix[..., :orbitals], axis1=-2, axis2=-1)  7.83 us
  transfers between devices with their start and end apart: 9, of which 9 were waited for; matrix products, arithmetic and copies ran while one was open for 4% of the time, Pallas kernels for 0%

profile of v1, /device:TPU:0, one launch (start us, length us, event | category | flops | bytes accessed | tf_op | source)
XLA Modules:
  0.0 268.2 jit_solution(11060126413458793453)
XLA Ops:
  6.5 3.0 %collective-permute-start = (f32[8,64,128]{2,1,0:T(8,128)}, f32[8,64,128]{2,1,0:T(8,128)S(1)}, u32[]{:S(2)}, u32[]{:S(2)}) collective-permute-start(f32[8,64,128]{2,1,0:T(8,128)} %param.7), channel_id=1, source_target_pairs={{0,4},{4,8},{8,12},{12,16},{16,20},{20,24},{24,28},{28,0},{1,5},{5... | collective-permute-start | bytes 786440 | tf_op jit(solution)/shard_map/ppermute | solution.py:92
  9.5 9.5 %collective-permute-done = f32[8,64,128]{2,1,0:T(8,128)S(1)} collective-permute-done((f32[8,64,128]{2,1,0:T(8,128)}, f32[8,64,128]{2,1,0:T(8,128)S(1)}, u32[]{:S(2)}, u32[]{:S(2)}) %collective-permute-start) | collective-permute-done | bytes 262176 | tf_op jit(solution)/shard_map/ppermute | solution.py:92
  19.1 10.1 %collective-permute-done.1 = f32[8,64,128]{2,1,0:T(8,128)S(1)} collective-permute-done((f32[8,64,128]{2,1,0:T(8,128)S(1)}, f32[8,64,128]{2,1,0:T(8,128)S(1)}, u32[]{:S(2)}, u32[]{:S(2)}) %collective-permute-start.1) | collective-permute-done | bytes 262176 | tf_op jit(solution)/shard_map/ppermute | solution.py:92
  29.3 9.2 %collective-permute-done.2 = f32[8,64,128]{2,1,0:T(8,128)S(1)} collective-permute-done((f32[8,64,128]{2,1,0:T(8,128)S(1)}, f32[8,64,128]{2,1,0:T(8,128)S(1)}, u32[]{:S(2)}, u32[]{:S(2)}) %collective-permute-start.2) | collective-permute-done | bytes 262176 | tf_op jit(solution)/shard_map/ppermute | solution.py:92
  38.7 0.2 sub.66
  38.9 1.0 constant_dynamic-update-slice_fusion.7
  39.9 7.7 %collective-permute-done.3 = f32[8,64,128]{2,1,0:T(8,128)S(1)} collective-permute-done((f32[8,64,128]{2,1,0:T(8,128)S(1)}, f32[8,64,128]{2,1,0:T(8,128)S(1)}, u32[]{:S(2)}, u32[]{:S(2)}) %collective-permute-start.3) | collective-permute-done | bytes 262176 | tf_op jit(solution)/shard_map/ppermute | solution.py:92
  47.6 1.4 fusion.62
  49.1 2.6 copy.25
  51.6 2.6 copy.27
  54.3 0.8 gather_fusion
  55.1 1.6 collective-permute-done.4
  56.9 9.8 %collective-permute-done.5 = f32[8,64,128]{2,1,0:T(8,128)S(1)} collective-permute-done((f32[8,64,128]{2,1,0:T(8,128)}, f32[8,64,128]{2,1,0:T(8,128)S(1)}, u32[]{:S(2)}, u32[]{:S(2)}) %collective-permute-start.5) | collective-permute-done | bytes 262176 | tf_op jit(solution)/shard_map/ppermute | solution.py:92
  66.7 1.0 constant_dynamic-update-slice_fusion.2
  67.7 8.0 %collective-permute-done.6 = f32[8,64,128]{2,1,0:T(8,128)S(1)} collective-permute-done((f32[8,64,128]{2,1,0:T(8,128)S(1)}, f32[8,64,128]{2,1,0:T(8,128)S(1)}, u32[]{:S(2)}, u32[]{:S(2)}) %collective-permute-start.6) | collective-permute-done | bytes 262176 | tf_op jit(solution)/shard_map/ppermute | solution.py:92
  75.8 2.7 %copy.26 = f32[64,64,128]{0,2,1:T(8,128)} copy(f32[64,64,128]{2,1,0:T(8,128)S(1)} %constant_dynamic-update-slice_fusion) | data formatting | bytes 4194304 | tf_op jit(solution)/shard_map/dynamic_update_slice | solution.py:95
  78.5 22.3 %subtract_subtract_fusion = f32[2,64,64,128]{1,0,3,2:T(2,128)} fusion(f32[2,64,128]{0,2,1:T(8,128)} %copy.27, f32[64,64,128]{0,2,1:T(8,128)} %copy.26, f32[2,64,128]{0,2,1:T(8,128)} %copy.25), kind=kLoop, calls=%fused_computation.30 | loop fusion | flops 2097152 | bytes 6422528 | tf_op jit(solution)/shard_map/sub | solution.py:31
  100.8 7.8 %fusion.63 = (f32[2,64,64,64]{1,0,3,2:T(2,128)}, f32[2,64,64,64]{1,0,3,2:T(2,128)}) fusion(f32[2,64,64,128]{1,0,3,2:T(2,128)} %subtract_subtract_fusion), kind=kLoop, calls=%fused_computation.103 | loop fusion | bytes 8388608 | tf_op jit(solution)/shard_map/slice | solution.py:36
  108.6 2.9 %gather_fusion.2 = f32[64,2,64]{2,1,0:T(2,128)S(1)} fusion(f32[2,64,64,64]{1,0,3,2:T(2,128)} %get-tuple-element.84, s32[64]{0:T(128)S(1)} %get-tuple-element.92), kind=kCustom, calls=%fused_computation.2 | custom fusion | bytes 66048 | tf_op jit(solution)/shard_map/jit(diagonal)/gather | solution.py:37
  111.7 3.0 %gather_fusion.1 = f32[64,2,64]{2,1,0:T(2,128)S(1)} fusion(f32[2,64,64,64]{1,0,3,2:T(2,128)} %get-tuple-element.83, s32[64]{0:T(128)S(1)} %get-tuple-element.92), kind=kCustom, calls=%fused_computation.1 | custom fusion | bytes 66048 | tf_op jit(solution)/shard_map/jit(diagonal)/gather | solution.py:36
  114.7 2.3 multiply_subtract_fusion
  117.1 3.1 %pad_maximum_fusion = f32[2,64,64,128]{3,2,1,0:T(8,128)} fusion(f32[2,64,64,64]{3,2,1,0:T(8,128)S(1)} %get-tuple-element.86, f32[2,64,64,64]{3,2,1,0:T(8,128)S(1)} %get-tuple-element.85), kind=kLoop, calls=%fused_computation.31 | loop fusion | flops 1048576 | bytes 8388608 | tf_op jit(solution)/shard_map/concatenate | solution.py:45
  120.2 87.5 %while.11 = (s32[]{:T(128)}, f32[2,64,64,128]{3,2,1,0:T(8,128)}, s32[]{:T(128)}, s32[2]{0:T(128)S(1)}, f32[64,128]{1,0:T(8,128)S(1)}, /*index=5*/f32[64,64,128]{...) while((s32[]{:T(128)}, f32[2,64,64,128]{3,2,1,0:T(8,128)}, ...), condition=%wide.region_2.3_spmd.clone, body=%wide.region_1.2_spmd.clone.sunk | while | flops 3234856960 | bytes 56787048 | solution.py:62
  121.1 2.2 copy.59
  123.2 1.4 slice_negate_fusion.4
  124.7 9.0 %bitcast_subtract_fusion.2 = f32[2,64,64,128]{3,2,1,0:T(8,128)S(1)} fusion(f32[64,128]{1,0:T(8,128)S(1)} %get-tuple-element.173, f32[2,64,128]{2,1,0:T(8,128)S(1)} %get-tuple-element.176, f32[64,64,128]{2,1,0:T(8,128)S(1)} %get-tuple-element.174, f32[2,64,128]{2,1,0:T(8,128)S(1)} %get-tuple-element.175, ...), kind=kOutput, calls=%fused_computation.18.clone.1 | convolution fusion | flops 1617952768 | bytes 14843904 | tf_op jit(solution)/shard_map/while/body/...ij,...jl->...il/dot_general | solution.py:20
  133.7 3.5 %slice_negate_fusion.5 = (f32[2,64,64,64]{3,2,1,0:T(8,128)S(1)}, f32[2,64,64,64]{3,2,1,0:T(8,128)}) fusion(f32[2,64,64,128]{3,2,1,0:T(8,128)S(1)} %bitcast_subtract_fusion.2), kind=kLoop, calls=%fused_computation.16.clone.1 | loop fusion | flops 524288 | bytes 8388608 | tf_op jit(solution)/shard_map/while/body/neg | solution.py:15
  137.2 11.9 %bitcast_select_fusion.2 = f32[2,64,64,128]{3,2,1,0:T(8,128)} fusion(f32[2,64,64,128]{3,2,1,0:T(8,128)S(1)} %copy.59, f32[2,64,64,64]{3,2,1,0:T(8,128)} %get-tuple-element.149, f32[2,64,64,64]{3,2,1,0:T(8,128)S(1)} %get-tuple-element.150, f32[2,64,64,128]{3,2,1,0:T(8,128)S(1)} %bitcast_subtract_fusion.2, pred[2]{0:T(512)(128)(4,1)S(1)} %broadcast_compare_fusion.2), kind=kOutput, calls=%fused_computation.17.clone.1 | convolution fusion | flops 1615855616 | bytes 16777218 | tf_op jit(solution)/shard_map/while/body/...ij,...jl->...il/dot_general | solution.py:20
  149.9 2.2 copy.59
  152.0 1.4 slice_negate_fusion.4
  153.5 9.0 %bitcast_subtract_fusion.2 = f32[2,64,64,128]{3,2,1,0:T(8,128)S(1)} fusion(f32[64,128]{1,0:T(8,128)S(1)} %get-tuple-element.173, f32[2,64,128]{2,1,0:T(8,128)S(1)} %get-tuple-element.176, f32[64,64,128]{2,1,0:T(8,128)S(1)} %get-tuple-element.174, f32[2,64,128]{2,1,0:T(8,128)S(1)} %get-tuple-element.175, ...), kind=kOutput, calls=%fused_computation.18.clone.1 | convolution fusion | flops 1617952768 | bytes 14843904 | tf_op jit(solution)/shard_map/while/body/...ij,...jl->...il/dot_general | solution.py:20
  162.5 3.5 %slice_negate_fusion.5 = (f32[2,64,64,64]{3,2,1,0:T(8,128)S(1)}, f32[2,64,64,64]{3,2,1,0:T(8,128)}) fusion(f32[2,64,64,128]{3,2,1,0:T(8,128)S(1)} %bitcast_subtract_fusion.2), kind=kLoop, calls=%fused_computation.16.clone.1 | loop fusion | flops 524288 | bytes 8388608 | tf_op jit(solution)/shard_map/while/body/neg | solution.py:15
  166.0 11.9 %bitcast_select_fusion.2 = f32[2,64,64,128]{3,2,1,0:T(8,128)} fusion(f32[2,64,64,128]{3,2,1,0:T(8,128)S(1)} %copy.59, f32[2,64,64,64]{3,2,1,0:T(8,128)} %get-tuple-element.149, f32[2,64,64,64]{3,2,1,0:T(8,128)S(1)} %get-tuple-element.150, f32[2,64,64,128]{3,2,1,0:T(8,128)S(1)} %bitcast_subtract_fusion.2, pred[2]{0:T(512)(128)(4,1)S(1)} %broadcast_compare_fusion.2), kind=kOutput, calls=%fused_computation.17.clone.1 | convolution fusion | flops 1615855616 | bytes 16777218 | tf_op jit(solution)/shard_map/while/body/...ij,...jl->...il/dot_general | solution.py:20
  178.7 2.2 copy.59
  180.8 1.4 slice_negate_fusion.4
  182.3 9.0 %bitcast_subtract_fusion.2 = f32[2,64,64,128]{3,2,1,0:T(8,128)S(1)} fusion(f32[64,128]{1,0:T(8,128)S(1)} %get-tuple-element.173, f32[2,64,128]{2,1,0:T(8,128)S(1)} %get-tuple-element.176, f32[64,64,128]{2,1,0:T(8,128)S(1)} %get-tuple-element.174, f32[2,64,128]{2,1,0:T(8,128)S(1)} %get-tuple-element.175, ...), kind=kOutput, calls=%fused_computation.18.clone.1 | convolution fusion | flops 1617952768 | bytes 14843904 | tf_op jit(solution)/shard_map/while/body/...ij,...jl->...il/dot_general | solution.py:20
  191.3 3.5 %slice_negate_fusion.5 = (f32[2,64,64,64]{3,2,1,0:T(8,128)S(1)}, f32[2,64,64,64]{3,2,1,0:T(8,128)}) fusion(f32[2,64,64,128]{3,2,1,0:T(8,128)S(1)} %bitcast_subtract_fusion.2), kind=kLoop, calls=%fused_computation.16.clone.1 | loop fusion | flops 524288 | bytes 8388608 | tf_op jit(solution)/shard_map/while/body/neg | solution.py:15
  194.8 11.9 %bitcast_select_fusion.2 = f32[2,64,64,128]{3,2,1,0:T(8,128)} fusion(f32[2,64,64,128]{3,2,1,0:T(8,128)S(1)} %copy.59, f32[2,64,64,64]{3,2,1,0:T(8,128)} %get-tuple-element.149, f32[2,64,64,64]{3,2,1,0:T(8,128)S(1)} %get-tuple-element.150, f32[2,64,64,128]{3,2,1,0:T(8,128)S(1)} %bitcast_subtract_fusion.2, pred[2]{0:T(512)(128)(4,1)S(1)} %broadcast_compare_fusion.2), kind=kOutput, calls=%fused_computation.17.clone.1 | convolution fusion | flops 1615855616 | bytes 16777218 | tf_op jit(solution)/shard_map/while/body/...ij,...jl->...il/dot_general | solution.py:20
  207.7 9.2 %dot_general.18 = f32[2,64,2,64,64]{3,2,1,4,0:T(2,128)} reshape(f32[2,64,128,64]{2,1,3,0:T(8,128)} %bitcast.62) | data formatting | bytes 8388608 | tf_op jit(solution)/shard_map/k,fkij->fij/dot_general | solution.py:104
  216.9 12.3 %fusion.27 = f32[1,2,64,2,64]{4,0,3,2,1:T(1,128)S(1)} fusion(f32[2,64,2,64,64]{3,2,1,4,0:T(2,128)} %dot_general.18, s32[64]{0:T(128)S(1)} %gather_fusion, s32[]{:T(128)S(6)} %mul.158), kind=kOutput, calls=%fused_computation.28 | convolution fusion | flops 12584384 | bytes 4260100 | tf_op jit(solution)/shard_map/k,fkij->fij/dot_general | solution.py:104
  229.2 0.6 copy.32
  229.9 16.8 %reduce-scatter.2.cloned.1.call-done = f32[2,2,8,1,128]{4,2,1,0,3:T(8,128)} async-done(((f32[2,2,8,4,128]{4,2,1,0,3:T(8,128)}), f32[2,2,8,1,128]{4,2,1,0,3:T(8,128)}) %reduce-scatter.2.cloned.1.call-update) | async-done | bytes 16400 | tf_op jit(solution)/shard_map/reduce_scatter | solution.py:109
  246.7 1.3 copy.33
  248.1 5.5 %all-to-all-start = ((f32[2,2,8,1,128]{4,3,1,0,2:T(1,128)}), f32[2,2,8,1,128]{4,3,1,0,2:T(1,128)S(1)}, u32[]{:S(2)}, u32[]{:S(2)}) async-start(f32[2,2,8,1,128]{4,3,1,0,2:T(1,128)} %copy.33), calls=%async_computation.1 | async-start | bytes 32768 | tf_op jit(solution)/shard_map/all_to_all | solution.py:110
  253.6 0.7 convert_reduce_fusion
  254.2 5.9 %all-to-all-done = f32[2,2,8,1,128]{4,3,1,0,2:T(1,128)S(1)} async-done(((f32[2,2,8,1,128]{4,3,1,0,2:T(1,128)}), f32[2,2,8,1,128]{4,3,1,0,2:T(1,128)S(1)}, u32[]{:S(2)}, u32[]{:S(2)}) %all-to-all-start) | async-done | bytes 16416 | tf_op jit(solution)/shard_map/all_to_all | solution.py:110
  260.1 0.6 broadcast_divide_fusion
  260.8 0.6 copy.34
  (39 shorter events, 0.8 us)
Async XLA Ops:
  6.5 45.1 %copy-start.1 = (f32[2,64,128]{2,1,0:T(8,128)S(1)}, f32[2,64,128]{2,1,0:T(8,128)}, u32[]{:S(2)}) copy-start(f32[2,64,128]{2,1,0:T(8,128)} %param.8) | copy-start | bytes 196612
  6.5 240.2 %reduce-scatter.2.cloned.1.call-start = ((), (), s32[]{:S(2)}) async-start(), calls=%async_computation.2 | async-start | bytes 81920 | tf_op jit(solution)/shard_map/reduce_scatter | solution.py:109
  6.5 12.5 %collective-permute-start = (f32[8,64,128]{2,1,0:T(8,128)}, f32[8,64,128]{2,1,0:T(8,128)S(1)}, u32[]{:S(2)}, u32[]{:S(2)}) collective-permute-start(f32[8,64,128]{2,1,0:T(8,128)} %param.7), channel_id=1, source_target_pairs={{0,4},{4,8},{8,12},{12,16},{16,20},{20,24},{24,28},{28,0},{1,5},{5... | collective-permute-start | bytes 786440 | tf_op jit(solution)/shard_map/ppermute | solution.py:92
  19.1 10.2 %collective-permute-start.1 = (f32[8,64,128]{2,1,0:T(8,128)S(1)}, f32[8,64,128]{2,1,0:T(8,128)S(1)}, u32[]{:S(2)}, u32[]{:S(2)}) collective-permute-start(f32[8,64,128]{2,1,0:T(8,128)S(1)} %collective-permute-done), channel_id=1, source_target_pairs={{0,4},{4,8},{8,12},{12,16},{16,20},{20,24},{24,28},{28,0},{1,5},{5... | collective-permute-start | bytes 786440 | tf_op jit(solution)/shard_map/ppermute | solution.py:92
  29.2 9.3 %collective-permute-start.2 = (f32[8,64,128]{2,1,0:T(8,128)S(1)}, f32[8,64,128]{2,1,0:T(8,128)S(1)}, u32[]{:S(2)}, u32[]{:S(2)}) collective-permute-start(f32[8,64,128]{2,1,0:T(8,128)S(1)} %collective-permute-done.1), channel_id=1, source_target_pairs={{0,4},{4,8},{8,12},{12,16},{16,20},{20,24},{24,28},{28,0},{1,5},{5... | collective-permute-start | bytes 786440 | tf_op jit(solution)/shard_map/ppermute | solution.py:92
  38.5 9.1 %collective-permute-start.3 = (f32[8,64,128]{2,1,0:T(8,128)S(1)}, f32[8,64,128]{2,1,0:T(8,128)S(1)}, u32[]{:S(2)}, u32[]{:S(2)}) collective-permute-start(f32[8,64,128]{2,1,0:T(8,128)S(1)} %collective-permute-done.2), channel_id=1, source_target_pairs={{0,4},{4,8},{8,12},{12,16},{16,20},{20,24},{24,28},{28,0},{1,5},{5... | collective-permute-start | bytes 786440 | tf_op jit(solution)/shard_map/ppermute | solution.py:92
  47.6 9.2 %collective-permute-start.4 = (f32[8,64,128]{2,1,0:T(8,128)S(1)}, f32[8,64,128]{2,1,0:T(8,128)}, u32[]{:S(2)}, u32[]{:S(2)}) collective-permute-start(f32[8,64,128]{2,1,0:T(8,128)S(1)} %collective-permute-done.3), channel_id=1, source_target_pairs={{0,4},{4,8},{8,12},{12,16},{16,20},{20,24},{24,28},{28,0},{1,5},{5... | collective-permute-start | bytes 786440 | tf_op jit(solution)/shard_map/ppermute | solution.py:92
  49.1 5.2 %copy-start = (s32[256]{0:T(256)S(1)}, s32[256]{0:T(256)}, u32[]{:S(2)}) copy-start(s32[256]{0:T(256)} %param.10) | copy-start | bytes 3076
  49.1 6.0 %copy-start.2 = (f32[2,64,128]{2,1,0:T(8,128)S(1)}, f32[2,64,128]{2,1,0:T(8,128)}, u32[]{:S(2)}) copy-start(f32[2,64,128]{2,1,0:T(8,128)} %param.9) | copy-start | bytes 196612
  56.8 9.9 %collective-permute-start.5 = (f32[8,64,128]{2,1,0:T(8,128)}, f32[8,64,128]{2,1,0:T(8,128)S(1)}, u32[]{:S(2)}, u32[]{:S(2)}) collective-permute-start(f32[8,64,128]{2,1,0:T(8,128)} %collective-permute-done.4), channel_id=1, source_target_pairs={{0,4},{4,8},{8,12},{12,16},{16,20},{20,24},{24,28},{28,0},{1,5},{5... | collective-permute-start | bytes 786440 | tf_op jit(solution)/shard_map/ppermute | solution.py:92
  66.7 9.1 %collective-permute-start.6 = (f32[8,64,128]{2,1,0:T(8,128)S(1)}, f32[8,64,128]{2,1,0:T(8,128)S(1)}, u32[]{:S(2)}, u32[]{:S(2)}) collective-permute-start(f32[8,64,128]{2,1,0:T(8,128)S(1)} %collective-permute-done.5), channel_id=1, source_target_pairs={{0,4},{4,8},{8,12},{12,16},{16,20},{20,24},{24,28},{28,0},{1,5},{5... | collective-permute-start | bytes 786440 | tf_op jit(solution)/shard_map/ppermute | solution.py:92
  248.1 12.1 %all-to-all-start = ((f32[2,2,8,1,128]{4,3,1,0,2:T(1,128)}), f32[2,2,8,1,128]{4,3,1,0,2:T(1,128)S(1)}, u32[]{:S(2)}, u32[]{:S(2)}) async-start(f32[2,2,8,1,128]{4,3,1,0,2:T(1,128)} %copy.33), calls=%async_computation.1 | async-start | bytes 32768 | tf_op jit(solution)/shard_map/all_to_all | solution.py:110
Sparse Core Ops, SparseCore 0:
  230.0 16.6 reduce-scatter.1
